TPU v7x, 32 devices: a whole 2x2x4 slice. The times are simulated.
32 devices in a mesh: replica: 4 (over x, core), fsdp: 4 (over z), tensor: 2 (over y).
Axes of the slice: x: 2, y: 2, z: 4, core: 2. Of those that a mesh axis runs over, the one named last changes fastest.
Arguments:
- pseudo_grad: bfloat16 [4, 3072, 18432], P('replica', 'fsdp', 'tensor'), may hold values from -6 to 6
- compensation: float32 [4, 3072, 18432], P('replica', 'fsdp', 'tensor'), may hold values from -6 to 6
- params: float32 [3072, 18432], P(('fsdp', 'replica'), 'tensor'), may hold values from -6 to 6
- momentum: float32 [3072, 18432], P(('fsdp', 'replica'), 'tensor'), may hold values from -6 to 6
- probe: bfloat16 [256, 18432], P('fsdp', 'tensor'), may hold values from -0.046875 to 0.046875
Outputs:
- new_params: float32 [3072, 18432], P(('fsdp', 'replica'), 'tensor')
- new_momentum: float32 [3072, 18432], P(('fsdp', 'replica'), 'tensor')
- probe_out: bfloat16 [256, 3072], P('tensor', 'fsdp')
All inputs are finite; a program needn't handle non-finite values.
Results may differ from a plain program's by a relative error of at most 0.014.
Values may be sent and summed in bfloat16 or wider, within the bound.
A program may use at most 128 MiB of HBM per device.

v0:
```python
import jax
import jax.numpy as jnp
from jax import lax
from jax.sharding import PartitionSpec as P

outer_rate = 0.7
nesterov = 0.9


def per_device(pseudo_grad, compensation, params, momentum, probe):
    outgoing = (pseudo_grad[0].astype(jnp.float32) + compensation[0]).astype(jnp.bfloat16)
    summed = lax.psum_scatter(outgoing, "replica", scatter_dimension=0, tiled=True).astype(
        jnp.float32
    )
    average = summed / lax.axis_size("replica")
    new_momentum = nesterov * momentum + average
    new_params = params - outer_rate * (average + nesterov * new_momentum)
    weights = new_params.astype(jnp.bfloat16)
    partial_value = lax.dot_general(
        lax.all_gather(probe, "fsdp", axis=0, tiled=True),
        weights,
        (((1,), (1,)), ((), ())),
        preferred_element_type=jnp.float32,
    )
    column_part = lax.psum_scatter(
        partial_value.astype(jnp.bfloat16), "tensor", scatter_dimension=0, tiled=True
    )
    probe_out = lax.all_gather(column_part, "replica", axis=1, tiled=True)
    return (new_params, new_momentum, probe_out)


def solution(mesh):
    in_specs = (
        P("replica", "fsdp", "tensor"),
        P("replica", "fsdp", "tensor"),
        P(("fsdp", "replica"), "tensor"),
        P(("fsdp", "replica"), "tensor"),
        P("fsdp", "tensor"),
    )
    out_specs = (
        P(("fsdp", "replica"), "tensor"),
        P(("fsdp", "replica"), "tensor"),
        P("tensor", "fsdp"),
    )
    return jax.shard_map(
        per_device, mesh=mesh, in_specs=in_specs, out_specs=out_specs, check_vma=False
    )
```

profile of v0, /device:TPU:0, one launch (start us, length us, event | category | flops | bytes accessed | tf_op | source)
XLA Modules:
  0.0 184.0 jit_solution(18287381123376863664)
XLA Ops:
  8.0 0.0 reduce-scatter.5.cloned.1.call-start
  8.0 19.2 %fusion = bf16[768,9216]{1,0:T(8,128)(2,1)} fusion(f32[1,768,9216]{2,1,0:T(8,128)} %param.6, bf16[1,768,9216]{2,1,0:T(8,128)(2,1)} %param.5), kind=kLoop, calls=%fused_computation.1 | loop fusion | flops 21233664 | bytes 56623104 | tf_op jit(solution)/shard_map/convert_element_type | solution.py:11
  27.3 0.0 reduce-scatter.5.cloned.1.call-update
  27.3 0.0 all-gather.2.cloned.1.call-start
  27.3 0.5 all-gather.2.cloned.1.call-update
  27.9 0.0 reduce-scatter.7.cloned.1.call-start
  27.9 112.7 %reduce-scatter.5.cloned.1.call-done = bf16[192,9216]{1,0:T(8,128)(2,1)} async-done(((bf16[768,9216]{1,0:T(8,128)(2,1)}), bf16[192,9216]{1,0:T(8,128)(2,1)}) %reduce-scatter.5.cloned.1.call-update) | async-done | bytes 3538960 | tf_op jit(solution)/shard_map/reduce_scatter | solution.py:12
  140.6 11.2 %multiply_subtract_fusion = (f32[192,9216]{1,0:T(8,128)}, f32[192,9216]{1,0:T(8,128)}) fusion(f32[192,9216]{1,0:T(8,128)} %param.7, bf16[192,9216]{1,0:T(8,128)(2,1)} %reduce-scatter.5.cloned.1.call-done, f32[192,9216]{1,0:T(8,128)} %param.8), kind=kLoop, calls=%fused_computation.2 | loop fusion | flops 14155776 | bytes 31850496 | tf_op jit(solution)/shard_map/sub | solution.py:17
  151.9 0.0 all-gather.2.cloned.1.call-done
  151.9 6.1 %fusion.6 = bf16[256,192]{0,1:T(8,128)(2,1)S(1)} fusion(bf16[256,9216]{1,0:T(8,128)(2,1)} %all-gather.2.cloned.1.call-done, f32[192,9216]{1,0:T(8,128)} %get-tuple-element.9), kind=kOutput, calls=%fused_computation.8 | convolution fusion | flops 907788288 | bytes 11894784 | tf_op jit(solution)/shard_map/dot_general | solution.py:19
  158.0 0.8 copy.10
  158.7 0.0 reduce-scatter.7.cloned.1.call-update
  158.8 10.4 %reduce-scatter.7.cloned.1.call-done = bf16[128,192]{1,0:T(8,128)(2,1)} async-done(((bf16[256,192]{1,0:T(8,128)(2,1)}), bf16[128,192]{1,0:T(8,128)(2,1)}) %reduce-scatter.7.cloned.1.call-update) | async-done | bytes 49168
  169.2 0.9 copy.11
  170.1 5.6 %all_gather.7 = bf16[128,768]{0,1:T(8,128)(2,1)S(1)} all-gather(bf16[128,192]{0,1:T(8,128)(2,1)S(1)} %copy.11), channel_id=1, replica_groups=mesh['replica'=4,'fsdp'=4,'tensor'=2] {'replica'}, dimensions={1}, use_global_device_ids=true | all-gather | bytes 245760 | tf_op jit(solution)/shard_map/all_gather | solution.py:28
  175.7 0.8 copy.9
Async XLA Ops:
  8.0 132.7 %reduce-scatter.5.cloned.1.call-start = ((), (), s32[]{:S(2)}) async-start(), calls=%async_computation.2 | async-start | bytes 17694720 | tf_op jit(solution)/shard_map/reduce_scatter | solution.py:12
  27.3 124.6 %all-gather.2.cloned.1.call-start = ((), (), s32[]{:S(2)}) async-start(), calls=%async_computation.3 | async-start | bytes 5898240 | tf_op jit(solution)/shard_map/all_gather | solution.py:20
  27.9 141.3 %reduce-scatter.7.cloned.1.call-start = ((), (), s32[]{:S(2)}) async-start(), calls=%async_computation.4 | async-start | bytes 196608
Sparse Core Ops, SparseCore 0:
  27.4 113.2 reduce-scatter.4
Sparse Core Ops, SparseCore 1:
  29.3 91.9 all-gather.1
  158.8 10.3 reduce-scatter.6
where the time goes:
time: 184 us
  waiting for transfers between devices  124 us (67%)
  other arithmetic  30.5 us (17%)
  between operations  15.5 us (8%)
  matrix products  6.07 us (3%)
  blocking collectives  5.6 us (3%)
  local copies, waits for them, and re-layouts  2.53 us (1%)
    reduce_scatter x1, waiting for transfers between devices, per_device(): lax.psum_scatter(outgoing, 'replica', scatter_dimension=0, tiled=True)  113 us
    convert_element_type x1, other arithmetic, per_device(): (pseudo_grad[0].astype(jnp.float32) + compensation[0]).astype(jnp.bfloat16)  19.2 us
    sub x1, other arithmetic, per_device(): new_params = params - outer_rate * (average + nesterov * new_momentum)  11.2 us
    unnamed x4, waiting for transfers between devices  11 us
    dot_general x1, matrix products, per_device(): lax.dot_general(lax.all_gather(probe, 'fsdp', axis=0, tiled=True), weight...  6.07 us
    all_gather x1, blocking collectives, per_device(): probe_out = lax.all_gather(column_part, 'replica', axis=1, tiled=True)  5.6 us
  transfers between devices with their start and end apart: 3, of which 2 were waited for; matrix products, arithmetic and copies ran while one was open for 6% of the time, Pallas kernels for 0%

commit v1 on v0

v1 whole, which is shorter than its diff:
```python
import functools

import jax
import jax.numpy as jnp
from jax import lax
from jax.experimental import pallas as pl
from jax.experimental.pallas import tpu as pltpu
from jax.sharding import PartitionSpec as P


outer_rate = 0.7
nesterov = 0.9
f32, bf16 = jnp.float32, jnp.bfloat16


def chunk_edges(tiles):
    edges = [0]
    for share in (2 / 18, 6 / 18, 12 / 18, 16 / 18):
        edge = max(1, round(share * tiles))
        if edges[-1] < edge < tiles:
            edges.append(edge)
    return edges + [tiles]


def add_product(offsets, probes, weights, total):
    rows = jnp.concatenate([block[...] for block in probes], axis=0)
    product = lax.dot_general(
        rows, weights, (((1,), (1,)), ((), ())), preferred_element_type=f32
    )
    start = 0
    for i, block in enumerate(probes):
        height = block.shape[0]
        at = pl.ds(pl.multiple_of(offsets[1 + i], height), height)
        total[at, :] += product[start : start + height]
        start += height


def update_kernel(n_replica, n_arrived, n_probe, first, offsets, *refs):
    refs = list(refs)
    take = lambda n: [refs.pop(0) for _ in range(n)]
    grad, carried, params, momentum, mate = take(5)
    arrived = take(n_arrived)
    probes = take(n_probe)
    if not first:
        take(2)
    if n_probe:
        (before,) = take(1)
    elif not first:
        take(1)
    new_params, new_momentum, last = refs

    summed = grad[...].astype(f32) + carried[...] + mate[...].astype(f32)
    for part in arrived:
        summed += part[...].astype(f32)
    average = summed / n_replica
    moved = nesterov * momentum[...] + average
    updated = params[...] - outer_rate * (average + nesterov * moved)
    new_momentum[...] = moved
    new_params[...] = updated
    weights = updated.astype(bf16)
    if not n_probe:
        last[...] = weights
        return

    @pl.when(pl.program_id(0) == 0)
    def _():
        last[...] = before[...]

    add_product(offsets, probes, weights, last)


def product_kernel(offsets, *refs):
    *probes, weights, total = refs

    @pl.when(pl.program_id(0) == 0)
    def _():
        total[...] = jnp.zeros_like(total)

    add_product(offsets, probes, weights[...], total)


def call(kernel, offsets, steps, in_specs, args, out_specs, out_shape, aliases, area, n_rows, wide):
    return pl.pallas_call(
        kernel,
        grid_spec=pltpu.PrefetchScalarGridSpec(
            num_scalar_prefetch=1, grid=(steps,), in_specs=in_specs, out_specs=out_specs
        ),
        out_shape=out_shape,
        input_output_aliases=aliases,
        cost_estimate=pl.CostEstimate(
            flops=2 * area * n_rows, bytes_accessed=wide * area, transcendentals=0
        ),
        compiler_params=pltpu.CompilerParams(dimension_semantics=("arbitrary",)),
    )(offsets, *args)


def update(offsets, lo, hi, tile, n_replica, grad, carried, params, momentum, mate, arrived, probes, state, total):
    rows, columns = params.shape
    if lo % 2 == 0 and hi % 2 == 0 and not probes:
        lo, hi, tile = lo // 2, hi // 2, tile * 2
    there = pl.BlockSpec((rows, tile), lambda j, s: (0, lo + j))
    shard = pl.BlockSpec((None, rows, tile), lambda j, s: (0, s[0], lo + j))
    in_specs = [shard, shard, there, there, there]
    in_specs += [pl.BlockSpec((rows, tile), lambda j, s: (0, j))] * len(arrived)
    in_specs += [pl.BlockSpec((p.shape[0], tile), lambda j, s: (0, lo + j)) for p in probes]
    args = [grad, carried, params, momentum, mate, *arrived, *probes]
    hbm = pl.BlockSpec(memory_space=pl.ANY)
    aliases = {}
    if state is not None:
        kept = state[:2] if probes else state
        aliases = {1 + len(args) + i: i for i in range(len(kept))}
        in_specs += [hbm] * len(kept)
        args += kept
    full = jax.ShapeDtypeStruct((rows, columns), f32)
    n_rows = 0
    if probes:
        n_rows = total.shape[0]
        whole = pl.BlockSpec(total.shape, lambda j, s: (0, 0))
        in_specs.append(whole)
        args.append(total)
        last, last_shape = whole, jax.ShapeDtypeStruct(total.shape, f32)
    else:
        last, last_shape = there, jax.ShapeDtypeStruct((rows, columns), bf16)
    return call(
        functools.partial(update_kernel, n_replica, len(arrived), len(probes), state is None),
        offsets, hi - lo, in_specs, args, [there, there, last], [full, full, last_shape],
        aliases, rows * (hi - lo) * tile, n_rows, 26,
    )


def product(offsets, hi, tile, probes, weights):
    rows, _ = weights.shape
    n_rows = sum(p.shape[0] for p in probes)
    if hi % 2 == 0:
        hi, tile = hi // 2, tile * 2
    at = lambda j, s: (0, j)
    in_specs = [pl.BlockSpec((p.shape[0], tile), at) for p in probes]
    in_specs.append(pl.BlockSpec((rows, tile), at))
    return call(
        product_kernel, offsets, hi, in_specs, [*probes, weights],
        pl.BlockSpec((n_rows, rows), lambda j, s: (0, 0)),
        jax.ShapeDtypeStruct((n_rows, rows), f32), {}, rows * hi * tile, n_rows, 4,
    )


def start_gather(probe, core):
    n = lax.axis_size("fsdp")
    if n > 4:
        return [lax.all_gather(probe, "fsdp", axis=0, tiled=True)]
    half = probe.shape[0] // 2
    mine = lax.dynamic_slice_in_dim(probe, core * half, half, 0)
    return [
        lax.ppermute(mine, "fsdp", [(i, (i + step) % n) for i in range(n)])
        for step in range(1, n)
    ]


def end_gather(probe, fetched, core, partner):
    n = lax.axis_size("fsdp")
    if n > 4:
        return fetched, [jnp.int32(0)]
    here = lax.axis_index("fsdp")
    height = probe.shape[0]
    half = height // 2
    blocks, places = [probe], [here * height]
    for step, block in enumerate(fetched, 1):
        start = (here - step) % n * height
        blocks += [block, lax.ppermute(block, "replica", partner)]
        places += [start + core * half, start + (1 - core) * half]
    return blocks, places


def per_device(pseudo_grad, compensation, params, momentum, probe):
    n = lax.axis_size("replica")
    chips = n // 2
    me = lax.axis_index("replica")
    chip, core = me // 2, me % 2
    rows, columns = params.shape
    tile = 512 if columns % 512 == 0 else 128
    edges = chunk_edges(columns // tile)
    partner = [(i, i ^ 1) for i in range(n)]

    def outgoing(dest, lo, hi):
        where, size = (0, dest * rows, lo * tile), (1, rows, (hi - lo) * tile)
        grads = lax.dynamic_slice(pseudo_grad, where, size)[0]
        return grads.astype(f32) + lax.dynamic_slice(compensation, where, size)[0]

    order = me * 0

    def after(value):
        nonlocal order
        order, value = lax.optimization_barrier((order, value))
        return value

    spans = list(zip(edges, edges[1:]))

    def swap(i):
        lo, hi = spans[i]
        swapped = []
        for step in range(1, chips):
            there = (chip + step) % chips + order
            give = after(outgoing(there * 2 + 1 - core, lo, hi).astype(bf16))
            swapped.append(lax.ppermute(give, "replica", partner))
        return swapped

    def cross(i, swapped):
        lo, hi = spans[i]
        received = []
        for step, got in zip(range(1, chips), swapped):
            there = (chip + step) % chips + order
            part = outgoing(there * 2 + core, lo, hi) + got.astype(f32)
            part = after(part.astype(bf16))
            across = [(i, (i // 2 + step) % chips * 2 + i % 2) for i in range(n)]
            received.append(lax.ppermute(part, "replica", across))
        return received

    arrived = []
    swapped = swap(0)
    for i in range(len(spans)):
        following = swap(i + 1) if i + 1 < len(spans) else None
        arrived.append(cross(i, swapped))
        swapped = following
        if i == 0:
            fetched = start_gather(after(probe), core)
    own = (chip + order) * 2 + 1 - core
    give = after(outgoing(own, 0, edges[-1]).astype(bf16))
    mate = lax.ppermute(give, "replica", partner)
    blocks, places = end_gather(probe, fetched, core, partner)

    offsets = jnp.stack([me + order] + places).astype(jnp.int32)
    fused = len(spans) - 2
    state = total = None
    for i, ((lo, hi), received) in enumerate(zip(spans, arrived)):
        if i == fused:
            total = product(offsets, lo, tile, blocks, state[2])
        state = update(
            offsets, lo, hi, tile, n, pseudo_grad, compensation, params, momentum,
            mate, received, blocks if i >= fused else [], state, total,
        )
        if i >= fused:
            total = state[2]
    new_params, new_momentum, total = state

    splits = lax.axis_size("tensor")
    mine = lax.axis_index("tensor")
    height = total.shape[0] // splits
    piece = lambda which: lax.dynamic_slice_in_dim(total, which * height, height, 0)
    column_part = piece(mine)
    for step in range(1, splits):
        shift = [(i, (i + step) % splits) for i in range(splits)]
        sent = piece((mine + step) % splits).astype(bf16)
        column_part += lax.ppermute(sent, "tensor", shift).astype(f32)
    probe_out = lax.all_gather(column_part.astype(bf16), "replica", axis=1, tiled=True)
    return (new_params, new_momentum, probe_out)


def solution(mesh):
    in_specs = (
        P("replica", "fsdp", "tensor"),
        P("replica", "fsdp", "tensor"),
        P(("fsdp", "replica"), "tensor"),
        P(("fsdp", "replica"), "tensor"),
        P("fsdp", "tensor"),
    )
    out_specs = (
        P(("fsdp", "replica"), "tensor"),
        P(("fsdp", "replica"), "tensor"),
        P("tensor", "fsdp"),
    )

    return jax.shard_map(
        per_device, mesh=mesh, in_specs=in_specs, out_specs=out_specs, check_vma=False
    )
```

time: 184 us -> 154 us (0.84)
  waiting for transfers between devices: 124 us -> 50.4 us
  Pallas kernels: 0 us -> 34.6 us
  starting transfers between devices: 0.12 us -> 25.1 us
  between operations: 15.5 us -> 0.8 us
  matrix products: 6.07 us -> 0 us
  local copies, waits for them, and re-layouts: 2.53 us -> 5.68 us
    reduce_scatter x1 -> x0, waiting for transfers between devices: 113 us -> none  [per_device(): lax.psum_scatter(outgoing, 'replica', scatter_dimension=0, tiled=True)]
    ppermute x0 -> x18, waiting for transfers between devices: none -> 50.4 us  [the longest x5 34 us: cross(): received.append(lax.ppermute(part, 'replica', across))]
    pallas_call x0 -> x6, Pallas kernels: none -> 34.6 us  [call(): pl.pallas_call(kernel, grid_spec=pltpu.PrefetchScalarGridSpec(num_scalar_...]
    ppermute x0 -> x18, starting transfers between devices: none -> 25.1 us  [the longest x5 15 us: cross(): received.append(lax.ppermute(part, 'replica', across))]
    convert_element_type x1 -> x12, other arithmetic: 19.2 us -> 31.3 us  [the longest x5 13.5 us: cross(): part = after(part.astype(bf16))]
    sub x1 -> x0, other arithmetic: 11.2 us -> none  [per_device(): new_params = params - outer_rate * (average + nesterov * new_momentum)]
    unnamed x4 -> x0, waiting for transfers between devices: 11 us -> none
    dot_general x1 -> x0, matrix products: 6.07 us -> none  [per_device(): lax.dot_general(lax.all_gather(probe, 'fsdp', axis=0, tiled=True), weight...]
  transfers between devices with their start and end apart: 3 -> 18, of which waited for: 2 -> 3; matrix products, arithmetic and copies ran while one was open for 6% -> 14% of each run, Pallas kernels for 0% -> 20%
where the time goes in v1:
time: 154 us; the launch traced here: 153 us
  waiting for transfers between devices  50.4 us (33%)
  Pallas kernels  34.6 us (22%)
  other arithmetic  31.3 us (20%)
  starting transfers between devices  25.1 us (16%)
  local copies, waits for them, and re-layouts  5.68 us (4%)
  blocking collectives  5.6 us (4%)
    pallas_call x6, Pallas kernels, call(): pl.pallas_call(kernel, grid_spec=pltpu.PrefetchScalarGridSpec(num_scalar_...  34.6 us
    ppermute x5, waiting for transfers between devices, cross(): received.append(lax.ppermute(part, 'replica', across))  34 us
    ppermute x5, starting transfers between devices, cross(): received.append(lax.ppermute(part, 'replica', across))  15 us
    ppermute x3, waiting for transfers between devices, start_gather(): lax.ppermute(mine, 'fsdp', [(i, (i + step) % n) for i in range(n)])  13.6 us
    convert_element_type x5, other arithmetic, cross(): part = after(part.astype(bf16))  13.5 us
    convert_element_type x5, other arithmetic, swap(): give = after(outgoing(there * 2 + 1 - core, lo, hi).astype(bf16))  10.2 us
    convert_element_type x1, other arithmetic, per_device(): give = after(outgoing(own, 0, edges[-1]).astype(bf16))  6.62 us
    ppermute x3, starting transfers between devices, start_gather(): lax.ppermute(mine, 'fsdp', [(i, (i + step) % n) for i in range(n)])  6.13 us
  transfers between devices with their start and end apart: 18, of which 3 were waited for; matrix products, arithmetic and copies ran while one was open for 14% of the time, Pallas kernels for 20%

profile of v1, /device:TPU:0, one launch (start us, length us, event | category | flops | bytes accessed | tf_op | source)
XLA Modules:
  0.0 153.4 jit_solution(9353938884747265400)
XLA Ops:
  0.7 1.3 fusion.9
  2.6 2.7 %fusion.5 = bf16[192,2048]{1,0:T(8,128)(2,1)} fusion(f32[1,768,9216]{2,1,0:T(8,128)} %refs_1_.9, s32[]{:T(128)S(6)} %select_n.106, bf16[1,768,9216]{2,1,0:T(8,128)(2,1)} %refs_0_.11), kind=kLoop, calls=%fused_computation.12 | loop fusion | flops 1179648 | bytes 3145732 | tf_op jit(solution)/shard_map/convert_element_type | solution.py:202
  5.3 2.1 %fusion.8 = bf16[192,1024]{1,0:T(8,128)(2,1)} fusion(bf16[192,1024]{1,0:T(8,128)(2,1)S(1)} %collective-permute-done, f32[1,768,9216]{2,1,0:T(8,128)} %refs_1_.9, s32[]{:T(128)S(6)} %select_n.107, bf16[1,768,9216]{2,1,0:T(8,128)(2,1)} %refs_0_.11), kind=kLoop, calls=%fused_computation.17 | loop fusion | flops 983040 | bytes 1966084 | tf_op jit(solution)/shard_map/convert_element_type | solution.py:212
  7.4 2.2 %fusion.4 = bf16[192,3072]{1,0:T(8,128)(2,1)S(1)} fusion(f32[1,768,9216]{2,1,0:T(8,128)} %refs_1_.9, s32[]{:T(128)S(6)} %select_n.108, bf16[1,768,9216]{2,1,0:T(8,128)(2,1)} %refs_0_.11), kind=kLoop, calls=%fused_computation.11 | loop fusion | flops 1769472 | bytes 4718596 | tf_op jit(solution)/shard_map/convert_element_type | solution.py:202
  10.2 2.8 %fusion.3 = bf16[192,2048]{1,0:T(8,128)(2,1)} fusion(bf16[192,2048]{1,0:T(8,128)(2,1)S(1)} %collective-permute-done.1, f32[1,768,9216]{2,1,0:T(8,128)} %refs_1_.9, s32[]{:T(128)S(6)} %select_n.109, bf16[1,768,9216]{2,1,0:T(8,128)(2,1)} %refs_0_.11), kind=kLoop, calls=%fused_computation.8 | loop fusion | flops 1966080 | bytes 3932164 | tf_op jit(solution)/shard_map/convert_element_type | solution.py:212
  13.0 2.7 %fusion.6 = bf16[192,2048]{1,0:T(8,128)(2,1)} fusion(f32[1,768,9216]{2,1,0:T(8,128)} %refs_1_.9, s32[]{:T(128)S(6)} %select_n.110, bf16[1,768,9216]{2,1,0:T(8,128)(2,1)} %refs_0_.11), kind=kLoop, calls=%fused_computation.13 | loop fusion | flops 1179648 | bytes 3145732 | tf_op jit(solution)/shard_map/convert_element_type | solution.py:202
  15.8 3.5 %fusion.1 = bf16[192,3072]{1,0:T(8,128)(2,1)} fusion(bf16[192,3072]{1,0:T(8,128)(2,1)S(1)} %collective-permute-done.2, f32[1,768,9216]{2,1,0:T(8,128)} %refs_1_.9, s32[]{:T(128)S(6)} %select_n.111, bf16[1,768,9216]{2,1,0:T(8,128)(2,1)} %refs_0_.11), kind=kLoop, calls=%fused_computation.3 | loop fusion | flops 2949120 | bytes 5898244 | tf_op jit(solution)/shard_map/convert_element_type | solution.py:212
  19.2 1.3 fusion.10
  21.1 2.9 %fusion.2 = bf16[192,2048]{1,0:T(8,128)(2,1)} fusion(bf16[192,2048]{1,0:T(8,128)(2,1)S(1)} %collective-permute-done.3, f32[1,768,9216]{2,1,0:T(8,128)} %refs_1_.9, s32[]{:T(128)S(6)} %select_n.113, bf16[1,768,9216]{2,1,0:T(8,128)(2,1)} %refs_0_.11), kind=kLoop, calls=%fused_computation.6 | loop fusion | flops 1966080 | bytes 3932164 | tf_op jit(solution)/shard_map/convert_element_type | solution.py:212
  24.0 2.2 %fusion.7 = bf16[192,1024]{1,0:T(8,128)(2,1)} fusion(bf16[192,1024]{1,0:T(8,128)(2,1)S(1)} %collective-permute-done.4, f32[1,768,9216]{2,1,0:T(8,128)} %refs_1_.9, s32[]{:T(128)S(6)} %select_n.114, bf16[1,768,9216]{2,1,0:T(8,128)(2,1)} %refs_0_.11), kind=kLoop, calls=%fused_computation.15 | loop fusion | flops 983040 | bytes 1966084 | tf_op jit(solution)/shard_map/convert_element_type | solution.py:212
  26.2 6.6 %fusion = bf16[192,9216]{1,0:T(8,128)(2,1)} fusion(f32[1,768,9216]{2,1,0:T(8,128)} %refs_1_.9, s32[]{:T(128)S(6)} %select_n.115, bf16[1,768,9216]{2,1,0:T(8,128)(2,1)} %refs_0_.11), kind=kLoop, calls=%fused_computation.1 | loop fusion | flops 5308416 | bytes 14155780 | tf_op jit(solution)/shard_map/convert_element_type | solution.py:226
  32.9 1.1 constant_dynamic-slice_fusion
  34.0 4.1 %collective-permute-start.9 = (bf16[32,9216]{1,0:T(8,128)(2,1)S(1)}, bf16[32,9216]{1,0:T(8,128)(2,1)}, u32[]{:S(2)}, u32[]{:S(2)}) collective-permute-start(bf16[32,9216]{1,0:T(8,128)(2,1)S(1)} %constant_dynamic-slice_fusion), channel_id=1, source_target_pairs={{0,4},{2,6},{4,0},{6,2},{1,5},{3,7},{5,1},{7,3},{8,12},{10,14},{12... | collective-permute-start | bytes 1769480 | tf_op jit(solution)/shard_map/ppermute | solution.py:153
  38.1 1.5 collective-permute-start.14
  40.1 1.5 collective-permute-start.15
  41.6 34.0 %collective-permute-done.16.refs_5_ = bf16[192,1024]{1,0:T(8,128)(2,1)S(1)} collective-permute-done((bf16[192,1024]{1,0:T(8,128)(2,1)}, bf16[192,1024]{1,0:T(8,128)(2,1)S(1)}, u32[]{:S(2)}, u32[]{:S(2)}) %collective-permute-start.16) | collective-permute-done | bytes 393248 | tf_op jit(solution)/shard_map/ppermute | solution.py:214
  75.6 1.4 collective-permute-start.11
  77.6 13.6 %collective-permute-done.11.refs_5_.refs_11_ = bf16[32,9216]{1,0:T(8,128)(2,1)} collective-permute-done((bf16[32,9216]{1,0:T(8,128)(2,1)S(1)}, bf16[32,9216]{1,0:T(8,128)(2,1)}, u32[]{:S(2)}, u32[]{:S(2)}) %collective-permute-start.11) | collective-permute-done | bytes 589856 | tf_op jit(solution)/shard_map/ppermute | solution.py:153
  91.2 11.5 %collective-permute-start.13 = (bf16[192,2048]{1,0:T(8,128)(2,1)}, bf16[192,2048]{1,0:T(8,128)(2,1)}, u32[]{:S(2)}, u32[]{:S(2)}) collective-permute-start(bf16[192,2048]{1,0:T(8,128)(2,1)} %fusion.2), channel_id=1, source_target_pairs={{0,16},{8,24},{16,0},{24,8},{1,17},{9,25},{17,1},{25,9},{2,18},{10... | collective-permute-start | bytes 2359304 | tf_op jit(solution)/shard_map/ppermute | solution.py:214
  105.0 1.0 copy-done
  106.1 4.1 %shard_map.76 = (f32[192,9216]{1,0:T(8,128)}, f32[192,9216]{1,0:T(8,128)}, bf16[192,9216]{1,0:T(8,128)(2,1)}) custom-call(s32[8]{0:T(128)} %stack.35.offsets, bf16[1,768,9216]{2,1,0:T(8,128)(2,1)} %refs_0_.11, f32[1,768,9216]{2,1,0:T(8,128)} %refs_1_.9, f32[192,9216]{1,0:T(8,128)} %refs_2_.9, f32[192,9216]{1,0:T(8,128)} %refs_3_.9, ...), custom_call_target="tpu_custom_call" | custom-call | bytes 5111808 | tf_op jit(solution)/shard_map/pallas_call | solution.py:83
  110.2 5.3 %shard_map.77 = (f32[192,9216]{1,0:T(8,128)}, f32[192,9216]{1,0:T(8,128)}, bf16[192,9216]{1,0:T(8,128)(2,1)}) custom-call(s32[8]{0:T(128)} %stack.35.offsets, bf16[1,768,9216]{2,1,0:T(8,128)(2,1)} %refs_0_.11, f32[1,768,9216]{2,1,0:T(8,128)} %refs_1_.9, f32[192,9216]{1,0:T(8,128)} %refs_2_.9, ...), custom_call_target="tpu_custom_call", output_to_operand_aliasing={{0}: (7, {}), {1}: (8, {}), {2}: (9, {})} | custom-call | bytes 10223616 | tf_op jit(solution)/shard_map/pallas_call | solution.py:83
  115.5 8.0 %shard_map.78 = (f32[192,9216]{1,0:T(8,128)}, f32[192,9216]{1,0:T(8,128)}, bf16[192,9216]{1,0:T(8,128)(2,1)}) custom-call(s32[8]{0:T(128)} %stack.35.offsets, bf16[1,768,9216]{2,1,0:T(8,128)(2,1)} %refs_0_.11, f32[1,768,9216]{2,1,0:T(8,128)} %refs_1_.9, f32[192,9216]{1,0:T(8,128)} %refs_2_.9, ...), custom_call_target="tpu_custom_call", output_to_operand_aliasing={{0}: (7, {}), {1}: (8, {}), {2}: (9, {})} | custom-call | bytes 15335424 | tf_op jit(solution)/shard_map/pallas_call | solution.py:83
  123.5 6.5 %shard_map.79.refs_15_ = f32[256,192]{1,0:T(8,128)} custom-call(s32[8]{0:T(128)} %stack.35.offsets, bf16[64,9216]{1,0:T(8,128)(2,1)} %refs_6_.3, bf16[32,9216]{1,0:T(8,128)(2,1)} %collective-permute-done.7.refs_1_.refs_7_, bf16[32,9216]{1,0:T(8,128)(2,1)} %collective-permute-done.8.refs_2_.refs_8_, bf16[32,9216]{1,0:T(8,128)(2,1)} %collective-permute-done.9.refs_3_.refs_9_, ...), custom_call_target="tpu_custom_call" | custom-call | flops 603979776 | bytes 4718592 | tf_op jit(solution)/shard_map/pallas_call | solution.py:83
  130.0 6.5 %shard_map.80 = (f32[192,9216]{1,0:T(8,128)}, f32[192,9216]{1,0:T(8,128)}, f32[256,192]{1,0:T(8,128)}) custom-call(s32[8]{0:T(128)} %stack.35.offsets, bf16[1,768,9216]{2,1,0:T(8,128)(2,1)} %refs_0_.11, f32[1,768,9216]{2,1,0:T(8,128)} %refs_1_.9, f32[192,9216]{1,0:T(8,128)} %refs_2_.9, ...), custom_call_target="tpu_custom_call", output_to_operand_aliasing={{0}: (14, {}), {1}: (15, {})} | custom-call | flops 201326592 | bytes 10223616 | tf_op jit(solution)/shard_map/pallas_call | solution.py:83
  136.5 4.2 %shard_map.81 = (f32[192,9216]{1,0:T(8,128)}, f32[192,9216]{1,0:T(8,128)}, f32[256,192]{1,0:T(8,128)}) custom-call(s32[8]{0:T(128)} %stack.35.offsets, bf16[1,768,9216]{2,1,0:T(8,128)(2,1)} %refs_0_.11, f32[1,768,9216]{2,1,0:T(8,128)} %refs_1_.9, f32[192,9216]{1,0:T(8,128)} %refs_2_.9, ...), custom_call_target="tpu_custom_call", output_to_operand_aliasing={{0}: (14, {}), {1}: (15, {})} | custom-call | flops 100663296 | bytes 5111808 | tf_op jit(solution)/shard_map/pallas_call | solution.py:83
  140.7 0.9 dynamic-slice_convert_fusion
  141.7 1.6 %collective-permute-start.17 = (bf16[128,192]{1,0:T(8,128)(2,1)S(1)}, bf16[128,192]{1,0:T(8,128)(2,1)S(1)}, u32[]{:S(2)}, u32[]{:S(2)}) collective-permute-start(bf16[128,192]{1,0:T(8,128)(2,1)S(1)} %dynamic-slice_convert_fusion), channel_id=1, source_target_pairs={{0,1},{1,0},{2,3},{3,2},{4,5},{5,4},{6,7},{7,6},{8,9},{9,8},{10,11... | collective-permute-start | bytes 147464 | tf_op jit(solution)/shard_map/ppermute | solution.py:252
  143.2 2.8 %collective-permute-done.17 = bf16[128,192]{1,0:T(8,128)(2,1)S(1)} collective-permute-done((bf16[128,192]{1,0:T(8,128)(2,1)S(1)}, bf16[128,192]{1,0:T(8,128)(2,1)S(1)}, u32[]{:S(2)}, u32[]{:S(2)}) %collective-permute-start.17) | collective-permute-done | bytes 49184 | tf_op jit(solution)/shard_map/ppermute | solution.py:252
  146.0 0.9 add_convert_fusion.6
  147.0 5.6 %all_gather.3 = bf16[128,768]{0,1:T(8,128)(2,1)S(1)} all-gather(bf16[128,192]{0,1:T(8,128)(2,1)S(1)} %copy.18), channel_id=1, replica_groups=mesh['replica'=4,'fsdp'=4,'tensor'=2] {'replica'}, dimensions={1}, use_global_device_ids=true | all-gather | bytes 245760 | tf_op jit(solution)/shard_map/all_gather | solution.py:253
  152.6 0.8 copy.19
  (36 shorter events, 5.4 us)
Async XLA Ops:
  2.0 3.3 %collective-permute-start = (bf16[192,1024]{1,0:T(8,128)(2,1)S(1)}, bf16[192,1024]{1,0:T(8,128)(2,1)S(1)}, u32[]{:S(2)}, u32[]{:S(2)}) collective-permute-start(bf16[192,1024]{1,0:T(8,128)(2,1)S(1)} %fusion.9), channel_id=1, source_target_pairs={{0,8},{8,0},{16,24},{24,16},{1,9},{9,1},{17,25},{25,17},{2,10},{10... | collective-permute-start | bytes 1179656 | tf_op jit(solution)/shard_map/ppermute | solution.py:203
  5.2 5.0 %collective-permute-start.1 = (bf16[192,2048]{1,0:T(8,128)(2,1)}, bf16[192,2048]{1,0:T(8,128)(2,1)S(1)}, u32[]{:S(2)}, u32[]{:S(2)}) collective-permute-start(bf16[192,2048]{1,0:T(8,128)(2,1)} %fusion.5), channel_id=1, source_target_pairs={{0,8},{8,0},{16,24},{24,16},{1,9},{9,1},{17,25},{25,17},{2,10},{10... | collective-permute-start | bytes 2359304 | tf_op jit(solution)/shard_map/ppermute | solution.py:203
  9.7 6.1 %collective-permute-start.2 = (bf16[192,3072]{1,0:T(8,128)(2,1)S(1)}, bf16[192,3072]{1,0:T(8,128)(2,1)S(1)}, u32[]{:S(2)}, u32[]{:S(2)}) collective-permute-start(bf16[192,3072]{1,0:T(8,128)(2,1)S(1)} %fusion.4), channel_id=1, source_target_pairs={{0,8},{8,0},{16,24},{24,16},{1,9},{9,1},{17,25},{25,17},{2,10},{10... | collective-permute-start | bytes 3538952 | tf_op jit(solution)/shard_map/ppermute | solution.py:203
  15.7 5.4 %collective-permute-start.3 = (bf16[192,2048]{1,0:T(8,128)(2,1)}, bf16[192,2048]{1,0:T(8,128)(2,1)S(1)}, u32[]{:S(2)}, u32[]{:S(2)}) collective-permute-start(bf16[192,2048]{1,0:T(8,128)(2,1)} %fusion.6), channel_id=1, source_target_pairs={{0,8},{8,0},{16,24},{24,16},{1,9},{9,1},{17,25},{25,17},{2,10},{10... | collective-permute-start | bytes 2359304 | tf_op jit(solution)/shard_map/ppermute | solution.py:203
  20.6 3.4 %collective-permute-start.4 = (bf16[192,1024]{1,0:T(8,128)(2,1)S(1)}, bf16[192,1024]{1,0:T(8,128)(2,1)S(1)}, u32[]{:S(2)}, u32[]{:S(2)}) collective-permute-start(bf16[192,1024]{1,0:T(8,128)(2,1)S(1)} %fusion.10), channel_id=1, source_target_pairs={{0,8},{8,0},{16,24},{24,16},{1,9},{9,1},{17,25},{25,17},{2,10},{10... | collective-permute-start | bytes 1179656 | tf_op jit(solution)/shard_map/ppermute | solution.py:203
  32.8 70.5 %collective-permute-start.5 = (bf16[192,9216]{1,0:T(8,128)(2,1)}, bf16[192,9216]{1,0:T(8,128)(2,1)S(1)}, u32[]{:S(2)}, u32[]{:S(2)}) collective-permute-start(bf16[192,9216]{1,0:T(8,128)(2,1)} %fusion), channel_id=1, source_target_pairs={{0,8},{8,0},{16,24},{24,16},{1,9},{9,1},{17,25},{25,17},{2,10},{10... | collective-permute-start | bytes 10616840 | tf_op jit(solution)/shard_map/ppermute | solution.py:227
  34.0 42.9 %collective-permute-start.9 = (bf16[32,9216]{1,0:T(8,128)(2,1)S(1)}, bf16[32,9216]{1,0:T(8,128)(2,1)}, u32[]{:S(2)}, u32[]{:S(2)}) collective-permute-start(bf16[32,9216]{1,0:T(8,128)(2,1)S(1)} %constant_dynamic-slice_fusion), channel_id=1, source_target_pairs={{0,4},{2,6},{4,0},{6,2},{1,5},{3,7},{5,1},{7,3},{8,12},{10,14},{12... | collective-permute-start | bytes 1769480 | tf_op jit(solution)/shard_map/ppermute | solution.py:153
  38.1 65.2 %collective-permute-start.14 = (bf16[192,3072]{1,0:T(8,128)(2,1)}, bf16[192,3072]{1,0:T(8,128)(2,1)S(1)}, u32[]{:S(2)}, u32[]{:S(2)}) collective-permute-start(bf16[192,3072]{1,0:T(8,128)(2,1)} %fusion.1), channel_id=1, source_target_pairs={{0,16},{8,24},{16,0},{24,8},{1,17},{9,25},{17,1},{25,9},{2,18},{10... | collective-permute-start | bytes 3538952 | tf_op jit(solution)/shard_map/ppermute | solution.py:214
  39.6 36.0 %collective-permute-start.16 = (bf16[192,1024]{1,0:T(8,128)(2,1)}, bf16[192,1024]{1,0:T(8,128)(2,1)S(1)}, u32[]{:S(2)}, u32[]{:S(2)}) collective-permute-start(bf16[192,1024]{1,0:T(8,128)(2,1)} %fusion.8), channel_id=1, source_target_pairs={{0,16},{8,24},{16,0},{24,8},{1,17},{9,25},{17,1},{25,9},{2,18},{10... | collective-permute-start | bytes 1179656 | tf_op jit(solution)/shard_map/ppermute | solution.py:214
  40.1 62.6 %collective-permute-start.15 = (bf16[192,2048]{1,0:T(8,128)(2,1)}, bf16[192,2048]{1,0:T(8,128)(2,1)S(1)}, u32[]{:S(2)}, u32[]{:S(2)}) collective-permute-start(bf16[192,2048]{1,0:T(8,128)(2,1)} %fusion.3), channel_id=1, source_target_pairs={{0,16},{8,24},{16,0},{24,8},{1,17},{9,25},{17,1},{25,9},{2,18},{10... | collective-permute-start | bytes 2359304 | tf_op jit(solution)/shard_map/ppermute | solution.py:214
  75.6 27.8 %copy-start.3 = (bf16[192,1024]{1,0:T(8,128)(2,1)}, bf16[192,1024]{1,0:T(8,128)(2,1)S(1)}, u32[]{:S(2)}) copy-start(bf16[192,1024]{1,0:T(8,128)(2,1)S(1)} %collective-permute-done.16.refs_5_) | copy-start | bytes 1179652
  75.6 15.7 %collective-permute-start.11 = (bf16[32,9216]{1,0:T(8,128)(2,1)S(1)}, bf16[32,9216]{1,0:T(8,128)(2,1)}, u32[]{:S(2)}, u32[]{:S(2)}) collective-permute-start(bf16[32,9216]{1,0:T(8,128)(2,1)S(1)} %constant_dynamic-slice_fusion), channel_id=1, source_target_pairs={{0,6},{2,0},{4,2},{6,4},{1,7},{3,1},{5,3},{7,5},{8,14},{10,8},{12,... | collective-permute-start | bytes 1769480 | tf_op jit(solution)/shard_map/ppermute | solution.py:153
  76.9 25.8 %collective-permute-start.7 = (bf16[32,9216]{1,0:T(8,128)(2,1)S(1)}, bf16[32,9216]{1,0:T(8,128)(2,1)}, u32[]{:S(2)}, u32[]{:S(2)}) collective-permute-start(bf16[32,9216]{1,0:T(8,128)(2,1)S(1)} %constant_dynamic-slice_fusion), channel_id=1, source_target_pairs={{0,2},{2,4},{4,6},{6,0},{1,3},{3,5},{5,7},{7,1},{8,10},{10,12},{12... | collective-permute-start | bytes 1769480 | tf_op jit(solution)/shard_map/ppermute | solution.py:153
  91.2 38.8 %collective-permute-start.13 = (bf16[192,2048]{1,0:T(8,128)(2,1)}, bf16[192,2048]{1,0:T(8,128)(2,1)}, u32[]{:S(2)}, u32[]{:S(2)}) collective-permute-start(bf16[192,2048]{1,0:T(8,128)(2,1)} %fusion.2), channel_id=1, source_target_pairs={{0,16},{8,24},{16,0},{24,8},{1,17},{9,25},{17,1},{25,9},{2,18},{10... | collective-permute-start | bytes 2359304 | tf_op jit(solution)/shard_map/ppermute | solution.py:214
  102.7 20.7 %collective-permute-start.10 = (bf16[32,9216]{1,0:T(8,128)(2,1)}, bf16[32,9216]{1,0:T(8,128)(2,1)}, u32[]{:S(2)}, u32[]{:S(2)}) collective-permute-start(bf16[32,9216]{1,0:T(8,128)(2,1)} %collective-permute-done.9.refs_3_.refs_9_), channel_id=1, source_target_pairs={{0,8},{8,0},{16,24},{24,16},{1,9},{9,1},{17,25},{25,17},{2,10},{10... | collective-permute-start | bytes 1769480 | tf_op jit(solution)/shard_map/ppermute | solution.py:168
  102.7 0.9 copy-start.2
  102.7 20.7 %collective-permute-start.12 = (bf16[32,9216]{1,0:T(8,128)(2,1)}, bf16[32,9216]{1,0:T(8,128)(2,1)}, u32[]{:S(2)}, u32[]{:S(2)}) collective-permute-start(bf16[32,9216]{1,0:T(8,128)(2,1)} %collective-permute-done.11.refs_5_.refs_11_), channel_id=1, source_target_pairs={{0,8},{8,0},{16,24},{24,16},{1,9},{9,1},{17,25},{25,17},{2,10},{10... | collective-permute-start | bytes 1769480 | tf_op jit(solution)/shard_map/ppermute | solution.py:168
  103.2 1.1 copy-start.1
  103.2 20.2 %collective-permute-start.8 = (bf16[32,9216]{1,0:T(8,128)(2,1)}, bf16[32,9216]{1,0:T(8,128)(2,1)}, u32[]{:S(2)}, u32[]{:S(2)}) collective-permute-start(bf16[32,9216]{1,0:T(8,128)(2,1)} %collective-permute-done.7.refs_1_.refs_7_), channel_id=1, source_target_pairs={{0,8},{8,0},{16,24},{24,16},{1,9},{9,1},{17,25},{25,17},{2,10},{10... | collective-permute-start | bytes 1769480 | tf_op jit(solution)/shard_map/ppermute | solution.py:168
  104.3 1.7 %copy-start = (bf16[192,9216]{1,0:T(8,128)(2,1)}, bf16[192,9216]{1,0:T(8,128)(2,1)S(1)}, u32[]{:S(2)}) copy-start(bf16[192,9216]{1,0:T(8,128)(2,1)S(1)} %collective-permute-done.5.refs_4_) | copy-start | bytes 10616836
  104.3 32.2 %collective-permute-start.6 = (bf16[192,1024]{1,0:T(8,128)(2,1)}, bf16[192,1024]{1,0:T(8,128)(2,1)}, u32[]{:S(2)}, u32[]{:S(2)}) collective-permute-start(bf16[192,1024]{1,0:T(8,128)(2,1)} %fusion.7), channel_id=1, source_target_pairs={{0,16},{8,24},{16,0},{24,8},{1,17},{9,25},{17,1},{25,9},{2,18},{10... | collective-permute-start | bytes 1179656 | tf_op jit(solution)/shard_map/ppermute | solution.py:214
  141.7 4.3 %collective-permute-start.17 = (bf16[128,192]{1,0:T(8,128)(2,1)S(1)}, bf16[128,192]{1,0:T(8,128)(2,1)S(1)}, u32[]{:S(2)}, u32[]{:S(2)}) collective-permute-start(bf16[128,192]{1,0:T(8,128)(2,1)S(1)} %dynamic-slice_convert_fusion), channel_id=1, source_target_pairs={{0,1},{1,0},{2,3},{3,2},{4,5},{5,4},{6,7},{7,6},{8,9},{9,8},{10,11... | collective-permute-start | bytes 147464 | tf_op jit(solution)/shard_map/ppermute | solution.py:252
